TPU v7x, 32 devices: a whole 2x2x4 slice. The times are simulated.
32 devices in a mesh: level: 4 (over x, core), body: 8 (over z, y).
Axes of the slice: x: 2, y: 2, z: 4, core: 2. Of those that a mesh axis runs over, the one named last changes fastest.
Arguments:
- state: float32 [4, 6, 8192], P('level', None, 'body'), may hold values from -14 to 14
- history: float32 [4, 3, 6, 8192], P('level', None, None, 'body'), may hold values from -6 to 6
- masses: float32 [8192], P('body'), may hold values from 0.25 to 4
Outputs:
- final_state: float32 [4, 6, 8192], P('level', None, 'body')
All inputs are finite; a program needn't handle non-finite values.
Results may differ from a plain program's by a relative error of at most 0.0001.
Values sent between devices are 32-bit elements; how exact they have to be, the bound alone decides.
A program may use at most 64 MiB of HBM per device.

v0:
```python
import functools

import jax
import jax.numpy as jnp
from jax import lax
from jax.experimental import pallas as pl
from jax.experimental.pallas import tpu as pltpu
from jax.sharding import PartitionSpec as P

STEPS = 4
SOFTEN = 0.05
DELTA = 0.05
COUPLING = 512.0
BF16 = jnp.bfloat16
F32 = jnp.float32


def split_in_three(x):
    high = x.astype(BF16).astype(F32)
    rest = x - high
    middle = rest.astype(BF16).astype(F32)
    return high, middle, rest - middle


def corrected(current, force, past, lower, level):
    oldest, middle, newest = past
    quadrature = (
        oldest / 24.0 - 5.0 * middle / 24.0 + 19.0 * newest / 24.0 + 9.0 * lower / 24.0
    )
    return jnp.where(
        level == 0,
        current + DELTA * force,
        current + DELTA * (force - newest) + DELTA * quadrature,
    )


def kernel(ring, levels, *refs):
    count = refs[0].shape[1]
    accumulators = []
    for side in range(2):
        accumulators += [pltpu.ACC(side)((256, 256), F32)] * 2
        accumulators += [pltpu.ACC(side)((16, 256), F32)] * (count // 512)

    def scoped(*held):
        each = len(held) // 2
        sides = (held[:each], held[each:])
        window(ring, levels, [s[:2] for s in sides], [s[2:] for s in sides], *refs)

    pl.run_scoped(scoped, *accumulators)


def window(
    ring, levels, far, near, state, history, masses, out,
    blocks, vel, acc, hist_v, hist_a, pos, t8, target_pieces, sums,
    pos_send, pos_recv, vel_send, vel_recv, acc_send, acc_recv,
):
    count = state.shape[1]
    level = lax.axis_index("level")
    me = lax.axis_index("body")
    up = lax.rem(level + 1, levels)
    down = lax.rem(level + levels - 1, levels)

    def peer(distance):
        return lax.rem(me + distance, ring)

    def pos_copy(step, distance):
        return pltpu.make_async_remote_copy(
            src_ref=blocks.at[step, me],
            dst_ref=blocks.at[step, me],
            send_sem=pos_send.at[step, distance],
            recv_sem=pos_recv.at[step, me],
            device_id=(level, lax.rem(me + ring - distance, ring)),
            device_id_type=pl.DeviceIdType.MESH,
        )

    def pos_arrival(step, owner):
        return pltpu.make_async_remote_copy(
            src_ref=blocks.at[step, owner],
            dst_ref=blocks.at[step, owner],
            send_sem=pos_send.at[step, 0],
            recv_sem=pos_recv.at[step, owner],
            device_id=(level, owner),
            device_id_type=pl.DeviceIdType.MESH,
        )

    def up_copy(source, target, send, recv, step):
        return pltpu.make_async_remote_copy(
            src_ref=source.at[step],
            dst_ref=target.at[step + 3],
            send_sem=send.at[step],
            recv_sem=recv.at[step],
            device_id=(up, me),
            device_id_type=pl.DeviceIdType.MESH,
        )

    def vel_copy(step):
        return up_copy(vel, hist_v, vel_send, vel_recv, step)

    def acc_copy(step):
        return up_copy(acc, hist_a, acc_send, acc_recv, step)

    def publish(step, p):
        blocks[step, me, 0:3] = p
        blocks[step, me, 3:4] = jnp.sum(p * p, axis=0, keepdims=True)
        blocks[step, me, 4:5] = jnp.ones((1, count), F32)
        blocks[step, me, 5:7] = jnp.zeros((2, count), F32)
        blocks[step, me, 7:8] = masses[...]

    def broadcast(step):
        def one(distance, carry):
            pos_copy(step, distance).start()
            return carry
        lax.fori_loop(1, ring, one, 0)

    barrier = pltpu.get_barrier_semaphore()

    def greet(distance, carry):
        pl.semaphore_signal(
            barrier, inc=1, device_id=(level, peer(distance)),
            device_id_type=pl.DeviceIdType.MESH,
        )
        return carry

    lax.fori_loop(1, ring, greet, 0)
    for other in (up, down):
        pl.semaphore_signal(
            barrier, inc=1, device_id=(other, me), device_id_type=pl.DeviceIdType.MESH
        )
    pos[...] = state[0:3]
    publish(0, state[0:3])
    vel[0] = state[3:6]
    for k in range(3):
        hist_v[k] = history[k, 0:3]
        hist_a[k] = history[k, 3:6]
    pl.semaphore_wait(barrier, ring + 1)
    broadcast(0)
    vel_copy(0).start()

    def next_velocity(step):
        acc_copy(step).wait_recv()
        past = (hist_a[step], hist_a[step + 1], hist_a[step + 2])
        vel[step + 1] = corrected(vel[step], acc[step], past, hist_a[step + 3], level)

    def next_position(step):
        vel_copy(step).wait_recv()
        past = (hist_v[step], hist_v[step + 1], hist_v[step + 2])
        pos[...] = corrected(pos[...], vel[step], past, hist_v[step + 3], level)

    def prepare_targets(step):
        t8[0:3] = -2.0 * blocks[step, me, 0:3]
        t8[3:4] = jnp.ones((1, count), F32)
        t8[4:5] = blocks[step, me, 3:4] + SOFTEN
        t8[5:8] = jnp.zeros((3, count), F32)
        high, middle, low = split_in_three(t8[...])
        target_pieces[...] = jnp.concatenate(
            [high, middle, high, low, high, middle], axis=0
        ).astype(BF16)

    tile = 256
    tiles = count // tile
    sides = 2

    def add_block(step, owner):
        source = blocks[step, owner]
        high, middle, low = split_in_three(source)
        rows = [high, high, middle, high, low, middle, jnp.zeros((80, count), F32)]
        left = jnp.concatenate(rows, axis=0).T.astype(BF16)
        left = jnp.concatenate([left, jnp.zeros((count, 128), BF16)], axis=1)
        moments = source * source[7:8]
        coarse = moments.astype(BF16).astype(F32)
        right = jnp.concatenate([coarse, moments - coarse], axis=0).astype(BF16)
        rounds = [(j, i) for j in range(tiles) for i in range(0, tiles, sides)]
        turn = [0] * sides

        def stage(value, side):
            register = turn[side] % 2
            turn[side] += 1
            pltpu.matmul_push_rhs(value, staging_register=register, mxu_index=side)
            return register

        def distances(index):
            j, i = rounds[index]
            for side in range(sides):
                at = (i + side) * tile
                pieces = jnp.concatenate(
                    [target_pieces[:, at:at + tile], jnp.zeros((tile - 48, tile), BF16)], axis=0
                )
                register = stage(pieces, side)
                pltpu.matmul_acc_lhs(
                    far[side][index % 2], left[j * tile:(j + 1) * tile], load_staged_rhs=register
                )

        def pulls(index):
            j, i = rounds[index]
            part = right[:, j * tile:(j + 1) * tile]
            for side in range(sides):
                inverse = lax.rsqrt(pltpu.matmul_pop(far[side][index % 2]))
                weight = inverse * inverse * inverse
                weight_high = weight.astype(BF16)
                weight_low = (weight - weight_high.astype(F32)).astype(BF16)
                for piece in (weight_high, weight_low):
                    register = stage(piece, side)
                    pltpu.matmul_acc_lhs(
                        near[side][i // sides], part, load_staged_rhs=register
                    )

        distances(0)
        for index in range(len(rounds)):
            if index + 1 < len(rounds):
                distances(index + 1)
            pulls(index)

    for side in range(sides):
        for used in far[side] + near[side]:
            pltpu.matmul_pop(used)

    def one_step(step, carry):
        prepare_targets(step)

        def one_block(k, inner):
            owner = peer(k)

            @pl.when((k == 1) & (step > 0))
            def _():
                acc_copy(step - 1).start()

            @pl.when((k == 3) & (step > 0))
            def _():
                next_velocity(step - 1)

            @pl.when((k == 4) & (step > 0))
            def _():
                vel_copy(step).start()

            @pl.when(k == 6)
            def _():
                next_position(step)

            @pl.when((k == 6) & (step < STEPS - 1))
            def _():
                publish(step + 1, pos[...])

            @pl.when((k == 7) & (step < STEPS - 1))
            def _():
                broadcast(step + 1)

            @pl.when(k > 0)
            def _():
                pos_arrival(step, owner).wait_recv()

            add_block(step, owner)
            return inner

        lax.fori_loop(0, ring, one_block, 0)
        for i in range(tiles):
            sums[:, i * tile:(i + 1) * tile] = pltpu.matmul_pop(near[i % sides][i // sides])
        total = sums[0:8] + sums[8:16]
        own = blocks[step, me, 0:3]
        acc[step] = (total[0:3] - own * total[4:5]) * (COUPLING / (count * ring))
        return carry

    lax.fori_loop(0, STEPS, one_step, 0)
    acc_copy(STEPS - 1).start()
    out[0:3] = pos[...]
    next_velocity(STEPS - 1)
    out[3:6] = vel[STEPS]

    def drain(step, carry):
        def one(distance, inner):
            pos_copy(step, distance).wait_send()
            return inner
        lax.fori_loop(1, ring, one, 0)
        vel_copy(step).wait_send()
        acc_copy(step).wait_send()
        return carry

    lax.fori_loop(0, STEPS, drain, 0)


def solution(mesh):
    ring = mesh.shape["body"]
    levels = mesh.shape["level"]

    def on_device(state, history, masses):
        count = state.shape[2]
        dma = pltpu.SemaphoreType.DMA
        result = pl.pallas_call(
            functools.partial(kernel, ring, levels),
            out_shape=jax.ShapeDtypeStruct((6, count), F32),
            in_specs=[pl.BlockSpec(memory_space=pltpu.VMEM)] * 3,
            out_specs=pl.BlockSpec(memory_space=pltpu.VMEM),
            scratch_shapes=[
                pltpu.VMEM((STEPS, ring, 8, count), F32),
                pltpu.VMEM((STEPS + 1, 3, count), F32),
                pltpu.VMEM((STEPS, 3, count), F32),
                pltpu.VMEM((STEPS + 3, 3, count), F32),
                pltpu.VMEM((STEPS + 3, 3, count), F32),
                pltpu.VMEM((3, count), F32),
                pltpu.VMEM((8, count), F32),
                pltpu.VMEM((48, count), BF16),
                pltpu.VMEM((16, count), F32),
                dma((STEPS, ring)),
                dma((STEPS, ring)),
                dma((STEPS,)),
                dma((STEPS,)),
                dma((STEPS,)),
                dma((STEPS,)),
            ],
            compiler_params=pltpu.CompilerParams(
                collective_id=0, has_side_effects=True, vmem_limit_bytes=48 * 1024 * 1024
            ),
        )(state[0], history[0], masses[None, :])
        return result[None]

    placed = (P("level", None, "body"), P("level", None, None, "body"), P("body"))
    return jax.shard_map(
        on_device, mesh=mesh, in_specs=placed, out_specs=P("level", None, "body"), check_vma=False
    )
```

profile of v0, /device:TPU:0, one launch (start us, length us, event | category | flops | bytes accessed | tf_op | source)
XLA Modules:
  0.0 62.2 jit_solution(18085817440150806824)
XLA Ops:
  0.0 0.7 %copy.10 = f32[1,6,1024]{2,1,0:T(8,128)S(1)} copy(f32[1,6,1024]{2,0,1:T(1,128)} %param.3) | data formatting | bytes 49152
  0.7 0.0 copy-start
  0.8 0.9 %copy.9 = f32[1,3,6,1024]{3,2,0,1:T(8,128)S(1)} copy(f32[1,3,6,1024]{3,0,2,1:T(1,128)} %param.4) | data formatting | bytes 147456
  1.7 0.0 copy-done
  1.7 59.9 %shard_map.37 = f32[6,1024]{1,0:T(8,128)S(1)} custom-call(f32[6,1024]{1,0:T(8,128)S(1)} %bitcast.10, f32[3,6,1024]{2,1,0:T(8,128)S(1)} %bitcast.8, f32[1,1024]{1,0:T(1,128)S(1)} %bitcast.11), custom_call_target="tpu_custom_call" | custom-call | tf_op jit(solution)/shard_map/pallas_call | solution.py:287
  61.6 0.6 %copy.4 = f32[1,6,1024]{2,0,1:T(1,128)} copy(f32[1,6,1024]{2,1,0:T(8,128)S(1)} %bitcast.9) | data formatting | bytes 49152 | tf_op jit(solution)/shard_map/broadcast_in_dim | solution.py:313
Async XLA Ops:
  0.7 0.9 %copy-start = (f32[1024]{0:T(1024)S(1)}, f32[1024]{0:T(1024)}, u32[]{:S(2)}) copy-start(f32[1024]{0:T(1024)} %param.5) | copy-start | bytes 12292
where the time goes:
time: 62.4 us; the launch traced here: 62.2 us
  Pallas kernels  59.9 us (96%)
  local copies, waits for them, and re-layouts  2.3 us (4%)
    pallas_call x1, Pallas kernels, on_device(): pl.pallas_call(functools.partial(kernel, ring, levels), out_shape=jax.Sha...  59.9 us
    unnamed x4, local copies, waits for them, and re-layouts  1.66 us

commit v1 on v0

v1 whole, which is shorter than its diff:
```python
import functools

import jax
import jax.numpy as jnp
from jax import lax
from jax.experimental import pallas as pl
from jax.experimental.pallas import tpu as pltpu
from jax.sharding import PartitionSpec as P

STEPS = 4
SOFTEN = 0.05
DELTA = 0.05
COUPLING = 512.0
BF16 = jnp.bfloat16
F32 = jnp.float32
TILE = 256
SIDES = 2
LEAD = 3


def split_in_three(x):
    high = x.astype(BF16).astype(F32)
    rest = x - high
    middle = rest.astype(BF16).astype(F32)
    return high, middle, rest - middle


def corrected(current, force, past, lower, level):
    oldest, middle, newest = past
    quadrature = (
        oldest / 24.0 - 5.0 * middle / 24.0 + 19.0 * newest / 24.0 + 9.0 * lower / 24.0
    )
    return jnp.where(
        level == 0,
        current + DELTA * force,
        current + DELTA * (force - newest) + DELTA * quadrature,
    )


def kernel(ring, levels, *refs):
    count = refs[0].shape[1]
    accumulators = []
    for side in range(SIDES):
        accumulators += [pltpu.ACC(side)((TILE, TILE), F32)] * 2
        accumulators += [pltpu.ACC(side)((16, TILE), F32)] * (count // TILE)

    def scoped(*held):
        each = len(held) // SIDES
        sides = (held[:each], held[each:])
        window(ring, levels, [s[:2] for s in sides], [s[2:] for s in sides], *refs)

    pl.run_scoped(scoped, *accumulators)


def window(
    ring, levels, far, near, state, history, masses, out,
    blocks, left_even, left_odd, right_even, right_odd, target_pieces, vel, acc, hist_v, hist_a, low_hist,
    pos, sums, target_rows, source_rows,
    pos_send, pos_recv, acc_send, acc_recv, low_send, low_recv,
):
    count = state.shape[1]
    tiles = count // TILE
    level = lax.axis_index("level")
    me = lax.axis_index("body")
    total_turns = STEPS * ring
    left = (left_even, left_odd)
    right = (right_even, right_odd)

    def above(distance):
        return lax.rem(level + distance, levels)

    def peer(k):
        half = (k + 1) // 2
        return lax.rem(me + ring + half * (2 * lax.rem(k, 2) - 1), ring)

    def pos_copy(step, k):
        return pltpu.make_async_remote_copy(
            src_ref=blocks.at[step, me, 0:4],
            dst_ref=blocks.at[step, me, 0:4],
            send_sem=pos_send.at[step, k],
            recv_sem=pos_recv.at[step, me],
            device_id=(level, peer(k)),
            device_id_type=pl.DeviceIdType.MESH,
        )

    def pos_arrival(step, owner):
        return pltpu.make_async_remote_copy(
            src_ref=blocks.at[step, owner, 0:4],
            dst_ref=blocks.at[step, owner, 0:4],
            send_sem=pos_send.at[step, 0],
            recv_sem=pos_recv.at[step, owner],
            device_id=(level, owner),
            device_id_type=pl.DeviceIdType.MESH,
        )

    def acc_copy(step, distance):
        target = (hist_a, low_hist)[distance - 1]
        return pltpu.make_async_remote_copy(
            src_ref=acc.at[step],
            dst_ref=target.at[step + 3],
            send_sem=acc_send.at[distance - 1, step],
            recv_sem=acc_recv.at[distance - 1, step],
            device_id=(above(distance), me),
            device_id_type=pl.DeviceIdType.MESH,
        )

    def low_copy():
        return pltpu.make_async_remote_copy(
            src_ref=vel.at[0],
            dst_ref=hist_v.at[3],
            send_sem=low_send.at[0],
            recv_sem=low_recv.at[0],
            device_id=(above(1), me),
            device_id_type=pl.DeviceIdType.MESH,
        )

    def low_hist_copy():
        return pltpu.make_async_remote_copy(
            src_ref=hist_a.at[0:3],
            dst_ref=low_hist.at[0:3],
            send_sem=low_send.at[1],
            recv_sem=low_recv.at[1],
            device_id=(above(1), me),
            device_id_type=pl.DeviceIdType.MESH,
        )

    def broadcast(step):
        def one(k, carry):
            pos_copy(step, k).start()
            return carry
        lax.fori_loop(1, ring, one, 0)

    barrier = pltpu.get_barrier_semaphore()

    def greet(k, carry):
        pl.semaphore_signal(
            barrier, inc=1, device_id=(level, peer(k)), device_id_type=pl.DeviceIdType.MESH
        )
        return carry

    lax.fori_loop(1, ring, greet, 0)

    def greet_level(distance, carry):
        pl.semaphore_signal(
            barrier, inc=1, device_id=(above(distance), me), device_id_type=pl.DeviceIdType.MESH
        )
        return carry

    lax.fori_loop(1, levels, greet_level, 0)
    pos[...] = state[0:3]
    blocks[0, me, 0:3] = state[0:3]
    for step in range(STEPS):
        blocks[step, me, 3:4] = masses[...]
    vel[0] = state[3:6]
    for k in range(3):
        hist_v[k] = history[k, 0:3]
        hist_a[k] = history[k, 3:6]
    pl.semaphore_wait(barrier, ring - 1 + levels - 1)
    broadcast(0)
    low_copy().start()
    low_hist_copy().start()

    def next_position(step):
        past = (hist_v[step], hist_v[step + 1], hist_v[step + 2])
        return corrected(pos[...], vel[step], past, hist_v[step + 3], level)

    def next_velocity(step):
        acc_copy(step, 1).wait_recv()
        past = (hist_a[step], hist_a[step + 1], hist_a[step + 2])
        vel[step + 1] = corrected(vel[step], acc[step], past, hist_a[step + 3], level)

    def next_low_velocity(step):
        acc_copy(step, 2).wait_recv()
        past = (low_hist[step], low_hist[step + 1], low_hist[step + 2])
        hist_v[step + 4] = corrected(
            hist_v[step + 3], hist_a[step + 3], past, low_hist[step + 3], level - 1
        )

    def publish(step):
        moved = next_position(step - 1)
        pos[...] = moved
        blocks[step, me, 0:3] = moved
        prepare_targets(step)

    def augmented(step, owner):
        p = blocks[step, owner, 0:3]
        return p, jnp.sum(p * p, axis=0, keepdims=True), blocks[step, owner, 3:4]

    def prepare_targets(step):
        p, square, _ = augmented(step, me)
        target_rows[0:3] = -2.0 * p
        target_rows[4:5] = square + SOFTEN
        high, middle, low = split_in_three(target_rows[...])
        target_pieces[lax.rem(step, 2)] = jnp.concatenate(
            [high, middle, high, low, high, middle], axis=0
        ).astype(BF16)

    def prepare_sources(slot, step, owner):
        p, square, mass = augmented(step, owner)
        source_rows[0:3] = p
        source_rows[3:4] = square
        source = source_rows[...]
        high, middle, low = split_in_three(source)
        rows = [high, high, middle, high, low, middle, jnp.zeros((80, count), F32)]
        left[slot][...] = jnp.concatenate(rows, axis=0).astype(BF16).T
        moments = source * mass
        coarse = moments.astype(BF16).astype(F32)
        right[slot][...] = jnp.concatenate([coarse, moments - coarse], axis=0).astype(BF16)

    rounds = [(j, i) for j in range(tiles) for i in range(tiles)]
    registers = [0] * SIDES

    def stage(value, side):
        register = registers[side]
        registers[side] = 1 - register
        pltpu.matmul_push_rhs(value, staging_register=register, mxu_index=side)
        return register

    def buffer(index):
        return far[index % SIDES][(index // SIDES) % 2]

    def distances(index, slot, step):
        j, i = rounds[index]
        at = i * TILE
        pieces = target_pieces[lax.rem(step, 2), :, at:at + TILE]
        pieces = jnp.concatenate([pieces, jnp.zeros((TILE - 48, TILE), BF16)], axis=0)
        lhs = left[slot][j * TILE:(j + 1) * TILE]
        lhs = jnp.concatenate([lhs, jnp.zeros((TILE, 128), BF16)], axis=1)
        register = stage(pieces, index % SIDES)
        pltpu.matmul_acc_lhs(buffer(index), lhs, load_staged_rhs=register)

    def pulls(index, slot):
        j, i = rounds[index]
        part = right[slot][:, j * TILE:(j + 1) * TILE]
        inverse = lax.rsqrt(pltpu.matmul_pop(buffer(index)))
        weight = inverse * inverse * inverse
        weight_high = weight.astype(BF16)
        weight_low = weight - weight_high.astype(F32)
        for side, piece in enumerate((weight_high, weight_low)):
            register = stage(piece, side)
            pltpu.matmul_acc_lhs(near[side][i], part, load_staged_rhs=register)

    def add_block(slot, step, next_step):
        for index in range(len(rounds)):
            ahead = index + LEAD
            if ahead < len(rounds):
                distances(ahead, slot, step)
            else:
                distances(ahead - len(rounds), 1 - slot, next_step)
            pulls(index, slot)

    for side in range(SIDES):
        for used in far[side] + near[side]:
            pltpu.matmul_pop(used)

    def finish(step):
        for i in range(tiles):
            high = pltpu.matmul_pop(near[0][i])
            sums[:, i * TILE:(i + 1) * TILE] = high + pltpu.matmul_pop(near[1][i])
        total = sums[0:8] + sums[8:16]
        own = blocks[step, me, 0:3]
        acc[step] = (total[0:3] - own * total[4:5]) * (COUPLING / (count * ring))

    target_rows[...] = jnp.zeros((8, count), F32)
    target_rows[3:4] = jnp.ones((1, count), F32)
    source_rows[...] = jnp.zeros((8, count), F32)
    source_rows[4:5] = jnp.ones((1, count), F32)
    prepare_targets(0)
    prepare_sources(0, 0, me)
    for index in range(LEAD):
        distances(index, 0, 0)

    def one_turn(turn, slot):
        step = turn // ring
        k = lax.rem(turn, ring)
        after = lax.rem(turn + 1, total_turns)
        next_step = after // ring
        next_k = lax.rem(after, ring)

        if slot == 1:
            @pl.when(k == 1)
            def _():
                @pl.when(step > 0)
                def _():
                    acc_copy(step - 1, 1).start()
                    acc_copy(step - 1, 2).start()

                @pl.when(step == 0)
                def _():
                    low_copy().wait_recv()
                    publish(1)

            @pl.when((k == 5) & (step > 0) & (step < STEPS - 1))
            def _():
                broadcast(step + 1)
        else:
            @pl.when((k == 2) & (step == 0))
            def _():
                low_hist_copy().wait_recv()
                broadcast(1)

            @pl.when((k == 4) & (step > 0))
            def _():
                next_velocity(step - 1)
                next_low_velocity(step - 1)

                @pl.when(step < STEPS - 1)
                def _():
                    publish(step + 1)

        @pl.when(next_k > 0)
        def _():
            pos_arrival(next_step, peer(next_k)).wait_recv()

        prepare_sources(1 - slot, next_step, peer(next_k))
        add_block(slot, step, next_step)

        if slot == 1:
            @pl.when(k == ring - 1)
            def _():
                finish(step)

    def two_turns(pair, carry):
        one_turn(2 * pair, 0)
        one_turn(2 * pair + 1, 1)
        return carry

    lax.fori_loop(0, total_turns // 2, two_turns, 0)
    for index in range(LEAD):
        pltpu.matmul_pop(buffer(index))
    acc_copy(STEPS - 1, 1).start()
    out[0:3] = next_position(STEPS - 1)
    next_velocity(STEPS - 1)
    out[3:6] = vel[STEPS]

    def drain(step, carry):
        def one(k, inner):
            pos_copy(step, k).wait_send()
            return inner
        lax.fori_loop(1, ring, one, 0)
        acc_copy(step, 1).wait_send()

        @pl.when(step < STEPS - 1)
        def _():
            acc_copy(step, 2).wait_send()

        return carry

    lax.fori_loop(0, STEPS, drain, 0)
    low_copy().wait_send()
    low_hist_copy().wait_send()


def solution(mesh):
    ring = mesh.shape["body"]
    levels = mesh.shape["level"]

    def on_device(state, history, masses):
        count = state.shape[2]
        dma = pltpu.SemaphoreType.DMA
        rows = pltpu.VMEM
        result = pl.pallas_call(
            functools.partial(kernel, ring, levels),
            out_shape=jax.ShapeDtypeStruct((6, count), F32),
            in_specs=[pl.BlockSpec(memory_space=pltpu.VMEM)] * 3,
            out_specs=pl.BlockSpec(memory_space=pltpu.VMEM),
            scratch_shapes=[
                rows((STEPS, ring, 8, count), F32),
                rows((count, 128), BF16),
                rows((count, 128), BF16),
                rows((16, count), BF16),
                rows((16, count), BF16),
                rows((2, 48, count), BF16),
                rows((STEPS + 1, 3, count), F32),
                rows((STEPS, 3, count), F32),
                rows((STEPS + 4, 3, count), F32),
                rows((STEPS + 3, 3, count), F32),
                rows((STEPS + 3, 3, count), F32),
                rows((3, count), F32),
                rows((16, count), F32),
                rows((8, count), F32),
                rows((8, count), F32),
                dma((STEPS, ring)),
                dma((STEPS, ring)),
                dma((2, STEPS)),
                dma((2, STEPS)),
                dma((2,)),
                dma((2,)),
            ],
            compiler_params=pltpu.CompilerParams(
                collective_id=0, has_side_effects=True, vmem_limit_bytes=48 * 1024 * 1024
            ),
        )(state[0], history[0], masses[None, :])
        return result[None]

    placed = (P("level", None, "body"), P("level", None, None, "body"), P("body"))
    return jax.shard_map(
        on_device, mesh=mesh, in_specs=placed, out_specs=P("level", None, "body"), check_vma=False
    )
```

time: 62.4 us -> 48.5 us (0.78)
  Pallas kernels: 59.9 us -> 45.9 us
    pallas_call x1, Pallas kernels: 59.9 us -> 45.9 us  [on_device(): pl.pallas_call(functools.partial(kernel, ring, levels), out_shape=jax.Sha...]
where the time goes in v1:
time: 48.5 us; the launch traced here: 48.2 us
  Pallas kernels  45.9 us (95%)
  local copies, waits for them, and re-layouts  2.3 us (5%)
    pallas_call x1, Pallas kernels, on_device(): pl.pallas_call(functools.partial(kernel, ring, levels), out_shape=jax.Sha...  45.9 us
    unnamed x4, local copies, waits for them, and re-layouts  1.66 us

profile of v1, /device:TPU:0, one launch (start us, length us, event | category | flops | bytes accessed | tf_op | source)
XLA Modules:
  0.0 48.2 jit_solution(7752322150712156639)
XLA Ops:
  0.0 0.7 %copy.10 = f32[1,6,1024]{2,1,0:T(8,128)S(1)} copy(f32[1,6,1024]{2,0,1:T(1,128)} %param.3) | data formatting | bytes 49152
  0.7 0.0 copy-start
  0.8 0.9 %copy.9 = f32[1,3,6,1024]{3,2,0,1:T(8,128)S(1)} copy(f32[1,3,6,1024]{3,0,2,1:T(1,128)} %param.4) | data formatting | bytes 147456
  1.7 0.0 copy-done
  1.7 45.9 %shard_map.37 = f32[6,1024]{1,0:T(8,128)S(1)} custom-call(f32[6,1024]{1,0:T(8,128)S(1)} %bitcast.10, f32[3,6,1024]{2,1,0:T(8,128)S(1)} %bitcast.8, f32[1,1024]{1,0:T(1,128)S(1)} %bitcast.11), custom_call_target="tpu_custom_call" | custom-call | tf_op jit(solution)/shard_map/pallas_call | solution.py:362
  47.6 0.6 %copy.4 = f32[1,6,1024]{2,0,1:T(1,128)} copy(f32[1,6,1024]{2,1,0:T(8,128)S(1)} %bitcast.9) | data formatting | bytes 49152 | tf_op jit(solution)/shard_map/broadcast_in_dim | solution.py:394
Async XLA Ops:
  0.7 0.9 %copy-start = (f32[1024]{0:T(1024)S(1)}, f32[1024]{0:T(1024)}, u32[]{:S(2)}) copy-start(f32[1024]{0:T(1024)} %param.5) | copy-start | bytes 12292

commit v2 on v1

--- a/solution.py
+++ b/solution.py
@@ -12,10 +12,13 @@
 DELTA = 0.05
 COUPLING = 512.0
 BF16 = jnp.bfloat16
+F8 = jnp.float8_e4m3fn
 F32 = jnp.float32
 TILE = 256
 SIDES = 2
 LEAD = 3
+SPAN = 8.0
+SQUARE_SPAN = 4096.0
 
 
 def split_in_three(x):
@@ -38,7 +41,7 @@
 
 
 def kernel(ring, levels, *refs):
-    count = refs[0].shape[1]
+    count = refs[0].shape[-1]
     accumulators = []
     for side in range(SIDES):
         accumulators += [pltpu.ACC(side)((TILE, TILE), F32)] * 2
@@ -55,10 +58,10 @@
 def window(
     ring, levels, far, near, state, history, masses, out,
     blocks, left_even, left_odd, right_even, right_odd, target_pieces, vel, acc, hist_v, hist_a, low_hist,
-    pos, sums, target_rows, source_rows,
-    pos_send, pos_recv, acc_send, acc_recv, low_send, low_recv,
+    sums, target_rows, source_rows,
+    pos_send, pos_recv, acc_send, acc_recv, low_send, low_recv, load_sem, told,
 ):
-    count = state.shape[1]
+    count = state.shape[-1]
     tiles = count // TILE
     level = lax.axis_index("level")
     me = lax.axis_index("body")
@@ -69,9 +72,18 @@
     def above(distance):
         return lax.rem(level + distance, levels)
 
+    line = ring // 2
+    rank = me // 2
+    half = lax.rem(me, 2)
+    edge = jnp.minimum(rank, line - 1 - rank)
+    near_count = 1 + 2 * (rank > 0).astype(jnp.int32) + 2 * (rank < line - 1).astype(jnp.int32)
+
     def peer(k):
-        half = (k + 1) // 2
-        return lax.rem(me + ring + half * (2 * lax.rem(k, 2) - 1), ring)
+        q = k // 2
+        swing = rank + (q + 1) // 2 * (2 * lax.rem(q, 2) - 1)
+        beyond = jnp.where(rank <= line - 1 - rank, q, line - 1 - q)
+        other = jnp.where(q <= 2 * edge, swing, beyond)
+        return 2 * other + lax.rem(half + k, 2)
 
     def pos_copy(step, k):
         return pltpu.make_async_remote_copy(
@@ -124,11 +136,11 @@
             device_id_type=pl.DeviceIdType.MESH,
         )
 
-    def broadcast(step):
+    def broadcast(step, first=1, last=ring):
         def one(k, carry):
             pos_copy(step, k).start()
             return carry
-        lax.fori_loop(1, ring, one, 0)
+        lax.fori_loop(first, last, one, 0)
 
     barrier = pltpu.get_barrier_semaphore()
 
@@ -138,7 +150,7 @@
         )
         return carry
 
-    lax.fori_loop(1, ring, greet, 0)
+    lax.fori_loop(1, near_count + 1, greet, 0)
 
     def greet_level(distance, carry):
         pl.semaphore_signal(
@@ -147,22 +159,25 @@
         return carry
 
     lax.fori_loop(1, levels, greet_level, 0)
-    pos[...] = state[0:3]
-    blocks[0, me, 0:3] = state[0:3]
-    for step in range(STEPS):
-        blocks[step, me, 3:4] = masses[...]
-    vel[0] = state[3:6]
+
+    loads = [(state.at[c], blocks.at[0, me, c:c + 1]) for c in range(3)]
+    loads += [(masses, blocks.at[0, me, 3:4])]
+    early = len(loads)
+    loads += [(state.at[3 + c], vel.at[0, c:c + 1]) for c in range(3)]
     for k in range(3):
-        hist_v[k] = history[k, 0:3]
-        hist_a[k] = history[k, 3:6]
-    pl.semaphore_wait(barrier, ring - 1 + levels - 1)
-    broadcast(0)
-    low_copy().start()
-    low_hist_copy().start()
+        loads += [(history.at[k, c], hist_v.at[k, c:c + 1]) for c in range(3)]
+        loads += [(history.at[k, 3 + c], hist_a.at[k, c:c + 1]) for c in range(3)]
+    loads = [
+        pltpu.make_async_copy(source, target, load_sem.at[n])
+        for n, (source, target) in enumerate(loads)
+    ]
+    for load in loads:
+        load.start()
 
     def next_position(step):
         past = (hist_v[step], hist_v[step + 1], hist_v[step + 2])
-        return corrected(pos[...], vel[step], past, hist_v[step + 3], level)
+        held = blocks[step, me, 0:3]
+        return corrected(held, vel[step], past, hist_v[step + 3], level)
 
     def next_velocity(step):
         acc_copy(step, 1).wait_recv()
@@ -177,9 +192,8 @@
         )
 
     def publish(step):
-        moved = next_position(step - 1)
-        pos[...] = moved
-        blocks[step, me, 0:3] = moved
+        blocks[step, me, 0:3] = next_position(step - 1)
+        blocks[step, me, 3:4] = blocks[0, me, 3:4]
         prepare_targets(step)
 
     def augmented(step, owner):
@@ -188,21 +202,30 @@
 
     def prepare_targets(step):
         p, square, _ = augmented(step, me)
-        target_rows[0:3] = -2.0 * p
-        target_rows[4:5] = square + SOFTEN
-        high, middle, low = split_in_three(target_rows[...])
-        target_pieces[lax.rem(step, 2)] = jnp.concatenate(
-            [high, middle, high, low, high, middle], axis=0
-        ).astype(BF16)
+        target_rows[0:3] = (-2.0 / SPAN) * p
+        target_rows[4:5] = (square + SOFTEN) * (1.0 / SQUARE_SPAN)
+        rest = target_rows[...]
+        pieces = []
+        for _ in range(8):
+            pieces.append(rest.astype(F8).astype(F32))
+            rest = (rest - pieces[-1]) * 16.0
+        pieces = pieces + pieces[:4] + pieces[:2] + [jnp.zeros((16, count), F32)]
+        target_pieces[lax.rem(step, 2)] = jnp.concatenate(pieces, axis=0).astype(F8)
 
     def prepare_sources(slot, step, owner):
         p, square, mass = augmented(step, owner)
-        source_rows[0:3] = p
+        source_rows[0:3] = p * SPAN
         source_rows[3:4] = square
         source = source_rows[...]
         high, middle, low = split_in_three(source)
-        rows = [high, high, middle, high, low, middle, jnp.zeros((80, count), F32)]
-        left[slot][...] = jnp.concatenate(rows, axis=0).astype(BF16).T
+        high, middle, low = [
+            jnp.concatenate([part, part * 0.0625], axis=0).astype(BF16)
+            for part in (high, middle, low)
+        ]
+        steps = [jnp.array(2.0 ** -(8 * k), BF16) for k in range(4)]
+        rows = [high] + [high * by for by in steps[1:]] + [middle, middle * steps[1], low]
+        rows.append(jnp.zeros((16, count), BF16))
+        left[slot][...] = jnp.concatenate(rows, axis=0).T
         moments = source * mass
         coarse = moments.astype(BF16).astype(F32)
         right[slot][...] = jnp.concatenate([coarse, moments - coarse], axis=0).astype(BF16)
@@ -223,7 +246,7 @@
         j, i = rounds[index]
         at = i * TILE
         pieces = target_pieces[lax.rem(step, 2), :, at:at + TILE]
-        pieces = jnp.concatenate([pieces, jnp.zeros((TILE - 48, TILE), BF16)], axis=0)
+        pieces = jnp.concatenate([pieces, jnp.zeros((TILE // 2, TILE), F8)], axis=0)
         lhs = left[slot][j * TILE:(j + 1) * TILE]
         lhs = jnp.concatenate([lhs, jnp.zeros((TILE, 128), BF16)], axis=1)
         register = stage(pieces, index % SIDES)
@@ -245,7 +268,7 @@
             ahead = index + LEAD
             if ahead < len(rounds):
                 distances(ahead, slot, step)
-            else:
+            elif next_step is not None:
                 distances(ahead - len(rounds), 1 - slot, next_step)
             pulls(index, slot)
 
@@ -259,16 +282,58 @@
             sums[:, i * TILE:(i + 1) * TILE] = high + pltpu.matmul_pop(near[1][i])
         total = sums[0:8] + sums[8:16]
         own = blocks[step, me, 0:3]
-        acc[step] = (total[0:3] - own * total[4:5]) * (COUPLING / (count * ring))
+        acc[step] = (total[0:3] * (1.0 / SPAN) - own * (total[4:5] * (1.0 / SQUARE_SPAN))) * (
+            COUPLING / (count * ring)
+        )
 
     target_rows[...] = jnp.zeros((8, count), F32)
     target_rows[3:4] = jnp.ones((1, count), F32)
     source_rows[...] = jnp.zeros((8, count), F32)
-    source_rows[4:5] = jnp.ones((1, count), F32)
+    source_rows[4:5] = jnp.full((1, count), SQUARE_SPAN, F32)
+    for load in loads[:early]:
+        load.wait()
     prepare_targets(0)
     prepare_sources(0, 0, me)
     for index in range(LEAD):
         distances(index, 0, 0)
+    for load in loads[early:]:
+        load.wait()
+    pl.semaphore_wait(barrier, near_count + levels - 1)
+    broadcast(0, 1, near_count + 1)
+    low_copy().start()
+    low_hist_copy().start()
+
+    def tell():
+        for side, step in enumerate((2, -2)):
+            @pl.when((rank < line - 1) if step > 0 else (rank > 0))
+            def _():
+                pl.semaphore_signal(
+                    told.at[side], inc=1, device_id=(level, me + step),
+                    device_id_type=pl.DeviceIdType.MESH,
+                )
+
+    def hear():
+        for side, step in enumerate((2, -2)):
+            @pl.when((rank > 0) if step > 0 else (rank < line - 1))
+            def _():
+                pl.semaphore_wait(told.at[side], 1)
+
+    tell()
+    add_block(0, 0, None)
+    hear()
+
+    def relay(_, carry):
+        tell()
+        hear()
+        return carry
+
+    lax.fori_loop(0, line - 3, relay, 0)
+    broadcast(0, near_count + 1, ring)
+    first = peer(1)
+    pos_arrival(0, first).wait_recv()
+    prepare_sources(1, 0, first)
+    for index in range(LEAD):
+        distances(index, 1, 0)
 
     def one_turn(turn, slot):
         step = turn // ring
@@ -278,23 +343,21 @@
         next_k = lax.rem(after, ring)
 
         if slot == 1:
-            @pl.when(k == 1)
-            def _():
-                @pl.when(step > 0)
-                def _():
-                    acc_copy(step - 1, 1).start()
-                    acc_copy(step - 1, 2).start()
-
-                @pl.when(step == 0)
-                def _():
-                    low_copy().wait_recv()
-                    publish(1)
+            @pl.when((k == 1) & (step > 0))
+            def _():
+                acc_copy(step - 1, 1).start()
+                acc_copy(step - 1, 2).start()
+
+            @pl.when((k == 3) & (step == 0))
+            def _():
+                low_copy().wait_recv()
+                publish(1)
 
             @pl.when((k == 5) & (step > 0) & (step < STEPS - 1))
             def _():
                 broadcast(step + 1)
         else:
-            @pl.when((k == 2) & (step == 0))
+            @pl.when((k == 4) & (step == 0))
             def _():
                 low_hist_copy().wait_recv()
                 broadcast(1)
@@ -321,17 +384,21 @@
                 finish(step)
 
     def two_turns(pair, carry):
-        one_turn(2 * pair, 0)
         one_turn(2 * pair + 1, 1)
+        one_turn(2 * pair + 2, 0)
         return carry
 
-    lax.fori_loop(0, total_turns // 2, two_turns, 0)
+    lax.fori_loop(0, total_turns // 2 - 1, two_turns, 0)
+    one_turn(total_turns - 1, 1)
     for index in range(LEAD):
         pltpu.matmul_pop(buffer(index))
     acc_copy(STEPS - 1, 1).start()
-    out[0:3] = next_position(STEPS - 1)
+    moved = next_position(STEPS - 1)
+    for c in range(3):
+        out[c] = moved[c:c + 1]
     next_velocity(STEPS - 1)
-    out[3:6] = vel[STEPS]
+    for c in range(3):
+        out[3 + c] = vel[STEPS, c:c + 1]
 
     def drain(step, carry):
         def one(k, inner):
@@ -361,8 +428,8 @@
         rows = pltpu.VMEM
         result = pl.pallas_call(
             functools.partial(kernel, ring, levels),
-            out_shape=jax.ShapeDtypeStruct((6, count), F32),
-            in_specs=[pl.BlockSpec(memory_space=pltpu.VMEM)] * 3,
+            out_shape=jax.ShapeDtypeStruct((6, 1, count), F32),
+            in_specs=[pl.BlockSpec(memory_space=pltpu.HBM)] * 3,
             out_specs=pl.BlockSpec(memory_space=pltpu.VMEM),
             scratch_shapes=[
                 rows((STEPS, ring, 8, count), F32),
@@ -370,13 +437,12 @@
                 rows((count, 128), BF16),
                 rows((16, count), BF16),
                 rows((16, count), BF16),
-                rows((2, 48, count), BF16),
+                rows((2, 128, count), F8),
                 rows((STEPS + 1, 3, count), F32),
                 rows((STEPS, 3, count), F32),
                 rows((STEPS + 4, 3, count), F32),
                 rows((STEPS + 3, 3, count), F32),
                 rows((STEPS + 3, 3, count), F32),
-                rows((3, count), F32),
                 rows((16, count), F32),
                 rows((8, count), F32),
                 rows((8, count), F32),
@@ -386,12 +452,16 @@
                 dma((2, STEPS)),
                 dma((2,)),
                 dma((2,)),
+                dma((25,)),
+                pltpu.SemaphoreType.REGULAR((2,)),
             ],
             compiler_params=pltpu.CompilerParams(
-                collective_id=0, has_side_effects=True, vmem_limit_bytes=48 * 1024 * 1024
+                collective_id=0, has_side_effects=True, vmem_limit_bytes=60 * 1024 * 1024
             ),
-        )(state[0], history[0], masses[None, :])
-        return result[None]
+        )(
+            state.reshape(6, 1, count), history.reshape(3, 6, 1, count), masses.reshape(1, count)
+        )
+        return result.reshape(1, 6, count)
 
     placed = (P("level", None, "body"), P("level", None, None, "body"), P("body"))
     return jax.shard_map(

time: 48.5 us -> 44.3 us (0.913)
  Pallas kernels: 45.9 us -> 42.7 us
  local copies, waits for them, and re-layouts: 2.3 us -> 1.35 us
    pallas_call x1, Pallas kernels: 45.9 us -> 42.7 us  [on_device(): pl.pallas_call(functools.partial(kernel, ring, levels), out_shape=jax.Sha...]
    broadcast_in_dim x1 -> x0, local copies, waits for them, and re-layouts: 0.63 us -> none  [on_device(): return result[None]]
    unnamed x4 -> x1, local copies, waits for them, and re-layouts: 1.66 us -> 1.35 us
where the time goes in v2:
time: 44.3 us; the launch traced here: 44 us
  Pallas kernels  42.7 us (96%)
  local copies, waits for them, and re-layouts  1.35 us (3%)
    pallas_call x1, Pallas kernels, on_device(): pl.pallas_call(functools.partial(kernel, ring, levels), out_shape=jax.Sha...  42.7 us
    unnamed x1, local copies, waits for them, and re-layouts  1.35 us

profile of v2, /device:TPU:0, one launch (start us, length us, event | category | flops | bytes accessed | tf_op | source)
XLA Modules:
  0.0 44.0 jit_solution(12174370729792797132)
XLA Ops:
  0.0 42.7 %shard_map.37 = f32[6,1,1024]{2,1,0:T(1,128)} custom-call(f32[6,1,1024]{2,1,0:T(1,128)} %bitcast.6, f32[3,6,1,1024]{3,2,1,0:T(1,128)} %bitcast.5, f32[1,1024]{1,0:T(1,128)} %bitcast.7), custom_call_target="tpu_custom_call" | custom-call | tf_op jit(solution)/shard_map/pallas_call | solution.py:429
  42.7 1.3 %copy.5 = f32[1,6,1024]{2,0,1:T(1,128)} copy(f32[1,6,1024]{2,0,1:T(1,128)} %bitcast.4) | data formatting | bytes 49152

commit v3 on v2

--- a/solution.py
+++ b/solution.py
@@ -76,7 +76,11 @@
     rank = me // 2
     half = lax.rem(me, 2)
     edge = jnp.minimum(rank, line - 1 - rank)
-    near_count = 1 + 2 * (rank > 0).astype(jnp.int32) + 2 * (rank < line - 1).astype(jnp.int32)
+
+    def within(pairs):
+        return 1 + 2 * (jnp.minimum(rank, pairs) + jnp.minimum(line - 1 - rank, pairs))
+
+    near_count = within(1)
 
     def peer(k):
         q = k // 2
@@ -263,8 +267,8 @@
             register = stage(piece, side)
             pltpu.matmul_acc_lhs(near[side][i], part, load_staged_rhs=register)
 
-    def add_block(slot, step, next_step):
-        for index in range(len(rounds)):
+    def add_block(slot, step, next_step, first=0, last=len(rounds)):
+        for index in range(first, last):
             ahead = index + LEAD
             if ahead < len(rounds):
                 distances(ahead, slot, step)
@@ -290,36 +294,40 @@
     target_rows[3:4] = jnp.ones((1, count), F32)
     source_rows[...] = jnp.zeros((8, count), F32)
     source_rows[4:5] = jnp.full((1, count), SQUARE_SPAN, F32)
+    def tell():
+        for side, step in enumerate((2, -2)):
+            @pl.when((rank < line - 1) if step > 0 else (rank > 0))
+            def _():
+                pl.semaphore_signal(
+                    told.at[side], inc=1, device_id=(level, me + step),
+                    device_id_type=pl.DeviceIdType.MESH,
+                )
+
+    def hear():
+        for side, step in enumerate((2, -2)):
+            @pl.when((rank > 0) if step > 0 else (rank < line - 1))
+            def _():
+                pl.semaphore_wait(told.at[side], 1)
+
     for load in loads[:early]:
         load.wait()
+    pl.semaphore_wait(barrier, near_count + levels - 1)
+    broadcast(0, 1, near_count + 1)
+    tell()
+    for load in loads[early:]:
+        load.wait()
+    low_copy().start()
+    low_hist_copy().start()
     prepare_targets(0)
     prepare_sources(0, 0, me)
     for index in range(LEAD):
         distances(index, 0, 0)
-    for load in loads[early:]:
-        load.wait()
-    pl.semaphore_wait(barrier, near_count + levels - 1)
-    broadcast(0, 1, near_count + 1)
-    low_copy().start()
-    low_hist_copy().start()
-
-    def tell():
-        for side, step in enumerate((2, -2)):
-            @pl.when((rank < line - 1) if step > 0 else (rank > 0))
-            def _():
-                pl.semaphore_signal(
-                    told.at[side], inc=1, device_id=(level, me + step),
-                    device_id_type=pl.DeviceIdType.MESH,
-                )
-
-    def hear():
-        for side, step in enumerate((2, -2)):
-            @pl.when((rank > 0) if step > 0 else (rank < line - 1))
-            def _():
-                pl.semaphore_wait(told.at[side], 1)
-
+    middle = len(rounds) // 2
+    add_block(0, 0, None, 0, middle)
+    hear()
+    broadcast(0, near_count + 1, within(2) + 1)
     tell()
-    add_block(0, 0, None)
+    add_block(0, 0, None, middle)
     hear()
 
     def relay(_, carry):
@@ -327,49 +335,54 @@
         hear()
         return carry
 
-    lax.fori_loop(0, line - 3, relay, 0)
-    broadcast(0, near_count + 1, ring)
+    lax.fori_loop(0, line - 4, relay, 0)
+    broadcast(0, within(2) + 1, ring)
     first = peer(1)
     pos_arrival(0, first).wait_recv()
     prepare_sources(1, 0, first)
     for index in range(LEAD):
         distances(index, 1, 0)
 
-    def one_turn(turn, slot):
+    def one_turn(turn, slot, last=False):
         step = turn // ring
         k = lax.rem(turn, ring)
         after = lax.rem(turn + 1, total_turns)
         next_step = after // ring
         next_k = lax.rem(after, ring)
 
-        if slot == 1:
-            @pl.when((k == 1) & (step > 0))
+        if slot == 0:
+            @pl.when((k == 0) & (step > 0))
             def _():
                 acc_copy(step - 1, 1).start()
                 acc_copy(step - 1, 2).start()
 
-            @pl.when((k == 3) & (step == 0))
-            def _():
-                low_copy().wait_recv()
-                publish(1)
-
-            @pl.when((k == 5) & (step > 0) & (step < STEPS - 1))
-            def _():
+            @pl.when((k == 4) & (step < STEPS - 1))
+            def _():
+                @pl.when(step == 0)
+                def _():
+                    low_hist_copy().wait_recv()
+
                 broadcast(step + 1)
         else:
-            @pl.when((k == 4) & (step == 0))
-            def _():
-                low_hist_copy().wait_recv()
-                broadcast(1)
-
-            @pl.when((k == 4) & (step > 0))
-            def _():
-                next_velocity(step - 1)
-                next_low_velocity(step - 1)
+            @pl.when(k == 3)
+            def _():
+                @pl.when(step == 0)
+                def _():
+                    low_copy().wait_recv()
+
+                @pl.when(step > 0)
+                def _():
+                    next_velocity(step - 1)
+                    next_low_velocity(step - 1)
 
                 @pl.when(step < STEPS - 1)
                 def _():
                     publish(step + 1)
+
+        if last:
+            add_block(slot, step, None)
+            finish(step)
+            return
 
         @pl.when(next_k > 0)
         def _():
@@ -389,9 +402,7 @@
         return carry
 
     lax.fori_loop(0, total_turns // 2 - 1, two_turns, 0)
-    one_turn(total_turns - 1, 1)
-    for index in range(LEAD):
-        pltpu.matmul_pop(buffer(index))
+    one_turn(total_turns - 1, 1, last=True)
     acc_copy(STEPS - 1, 1).start()
     moved = next_position(STEPS - 1)
     for c in range(3):
@@ -428,7 +439,7 @@
         rows = pltpu.VMEM
         result = pl.pallas_call(
             functools.partial(kernel, ring, levels),
-            out_shape=jax.ShapeDtypeStruct((6, 1, count), F32),
+            out_shape=pltpu.VMEM((6, 1, count), F32),
             in_specs=[pl.BlockSpec(memory_space=pltpu.HBM)] * 3,
             out_specs=pl.BlockSpec(memory_space=pltpu.VMEM),
             scratch_shapes=[

time: 44.3 us -> 42.5 us (0.959)
  Pallas kernels: 42.7 us -> 41.7 us
  local copies, waits for them, and re-layouts: 1.35 us -> 0.61 us
    pallas_call x1, Pallas kernels: 42.7 us -> 41.7 us  [on_device(): pl.pallas_call(functools.partial(kernel, ring, levels), out_shape=pltpu.V...]
    unnamed x1, local copies, waits for them, and re-layouts: 1.35 us -> 0.61 us
where the time goes in v3:
time: 42.5 us; the launch traced here: 42.3 us
  Pallas kernels  41.7 us (98%)
  local copies, waits for them, and re-layouts  0.61 us (1%)
    pallas_call x1, Pallas kernels, on_device(): pl.pallas_call(functools.partial(kernel, ring, levels), out_shape=pltpu.V...  41.7 us

profile of v3, /device:TPU:0, one launch (start us, length us, event | category | flops | bytes accessed | tf_op | source)
XLA Modules:
  0.0 42.3 jit_solution(4246007506798770384)
XLA Ops:
  0.0 41.7 %shard_map.37 = f32[6,1,1024]{2,1,0:T(1,128)S(1)} custom-call(f32[6,1,1024]{2,1,0:T(1,128)} %bitcast.6, f32[3,6,1,1024]{3,2,1,0:T(1,128)} %bitcast.5, f32[1,1024]{1,0:T(1,128)} %bitcast.7), custom_call_target="tpu_custom_call" | custom-call | tf_op jit(solution)/shard_map/pallas_call | solution.py:440
  41.7 0.6 %copy.5 = f32[1,6,1024]{2,0,1:T(1,128)} copy(f32[1,6,1024]{2,0,1:T(1,128)S(1)} %bitcast.4) | data formatting | bytes 49152
